TPU v7x, 16 devices: a whole 2x2x2 slice. The times are simulated.
16 devices in a mesh: tp: 2 (over z), dp: 8 (over y, x, core).
Axes of the slice: x: 2, y: 2, z: 2, core: 2. Of those that a mesh axis runs over, the one named last changes fastest.
Arguments:
- h_teacher: bfloat16 [32768, 4096], P('dp')
- h_student: bfloat16 [32768, 4096], P('dp')
- w_teacher: bfloat16 [4096, 4096], P(None, 'tp')
- w_student: bfloat16 [4096, 4096], P(None, 'tp')
Outputs:
- output 1: float32 [], replicated
- output 2: float32 [32768, 4096], P('dp')
- output 3: float32 [4096, 4096], P(None, 'tp')
All inputs are finite; a program needn't handle non-finite values.
Results may differ from a plain program's by a relative error of at most 0.001.
Values sent between devices are 32-bit elements.
A program may use at most 1 GiB of HBM per device.

v0:
```python
import jax
import jax.numpy as jnp
from jax import lax
from jax.sharding import PartitionSpec as P


def solution(mesh):
    dp_size = mesh.shape["dp"]

    def local_step(h_teacher, h_student, w_teacher, w_student):
        tok_total = h_teacher.shape[0] * dp_size
        z_teacher = jnp.dot(h_teacher, w_teacher, preferred_element_type=jnp.float32)
        z_student = jnp.dot(h_student, w_student, preferred_element_type=jnp.float32)
        local_max = jnp.stack([jnp.max(z_teacher, axis=1), jnp.max(z_student, axis=1)], axis=1)
        row_max = lax.pmax(local_max, "tp")
        shift_t = z_teacher - row_max[:, 0:1]
        shift_s = z_student - row_max[:, 1:2]
        exp_t = jnp.exp(shift_t)
        exp_s = jnp.exp(shift_s)
        local_sum = jnp.stack([jnp.sum(exp_t, axis=1), jnp.sum(exp_s, axis=1)], axis=1)
        row_sum = lax.psum(local_sum, "tp")
        log_sum = jnp.log(row_sum)
        prob_t = exp_t / row_sum[:, 0:1]
        prob_s = exp_s / row_sum[:, 1:2]
        kl_part = jnp.sum(prob_t * ((shift_t - log_sum[:, 0:1]) - (shift_s - log_sum[:, 1:2])))
        kl_loss = lax.psum(kl_part, ("tp", "dp")) / tok_total
        dz_student = ((prob_s - prob_t) / tok_total).astype(jnp.bfloat16)
        dh_part = lax.dot_general(dz_student, w_student, (((1,), (1,)), ((), ())),
                                  preferred_element_type=jnp.float32)
        dh_student = lax.psum(dh_part, "tp")
        dw_part = lax.dot_general(h_student, dz_student, (((0,), (0,)), ((), ())),
                                  preferred_element_type=jnp.float32)
        dw_student = lax.psum(dw_part, "dp")
        return kl_loss, dh_student, dw_student

    return jax.shard_map(
        local_step, mesh=mesh,
        in_specs=(P("dp", None), P("dp", None), P(None, "tp"), P(None, "tp")),
        out_specs=(P(), P("dp", None), P(None, "tp")),
        check_vma=False)
```

profile of v0, /device:TPU:0, one launch (start us, length us, event | category | flops | bytes accessed | tf_op | source)
XLA Modules:
  0.0 2291.9 jit_solution(15788696866171629555)
XLA Ops:
  7.2 0.0 all-reduce.5.cloned.1.call-start
  7.2 115.4 %fusion.3 = (f32[4096]{0:T(1024)}, f32[4096,2048]{0,1:T(8,128)}) fusion(bf16[4096,4096]{1,0:T(8,128)(2,1)} %param.5, bf16[4096,2048]{1,0:T(8,128)(2,1)} %param.7), kind=kOutput, calls=%fused_computation.11 | convolution fusion | flops 68727865344 | bytes 83902464 | tf_op jit(solution)/shard_map/dot_general | solution.py:13
  122.6 0.0 copy-start.1
  122.6 114.8 %fusion.4 = (f32[4096]{0:T(1024)S(1)}, f32[4096,2048]{0,1:T(8,128)}) fusion(bf16[4096,4096]{1,0:T(8,128)(2,1)} %param.4, bf16[4096,2048]{1,0:T(8,128)(2,1)} %param.6), kind=kOutput, calls=%fused_computation.12 | convolution fusion | flops 68727865344 | bytes 83902464 | tf_op jit(solution)/shard_map/dot_general | solution.py:12
  237.4 0.0 copy-done.1
  237.4 10.3 pmax.7
  247.7 0.0 copy-start
  247.8 13.6 exponential_reduce_fusion
  261.4 6.6 copy-done
  268.0 5.0 exponential_reduce_fusion.1
  273.1 6.9 psum.28
  280.1 31.6 %multiply_convert_fusion = (bf16[4096,2048]{0,1:T(8,128)(2,1)}, f32[]{:T(128)}) fusion(f32[4096,2048]{0,1:T(8,128)} %get-tuple-element.18, f32[4096,2048]{0,1:T(8,128)} %get-tuple-element.20, f32[4096]{0:T(1024)S(1)} %bitcast.26, f32[4096]{0:T(1024)S(1)} %bitcast.27, f32[4096]{0:T(1024)S(1)} %bitcast.23, f32[4096]{0:T(1024)S(1)} %bitcast.21, ...), kind=kLoop, calls=%fused_computation | loop fusion | flops 100663296 | bytes 83984384 | tf_op jit(solution)/shard_map/convert_element_type | solution.py:27
  311.7 78.3 %convolution_bitcast_fusion = f32[4096,2048]{0,1:T(8,128)} fusion(bf16[4096,2048]{0,1:T(8,128)(2,1)} %get-tuple-element.9, bf16[4096,4096]{1,0:T(8,128)(2,1)} %param.5), kind=kOutput, calls=%fused_computation.5 | convolution fusion | flops 68719476736 | bytes 83886080 | tf_op jit(solution)/shard_map/dot_general | solution.py:31
  390.0 0.0 all-reduce.5.cloned.1.call-update
  390.0 0.0 all-reduce.3.cloned.1.call-start
  390.0 79.4 %fusion.5 = f32[4096,4096]{1,0:T(8,128)} fusion(bf16[4096,2048]{0,1:T(8,128)(2,1)} %get-tuple-element.9, bf16[4096,2048]{1,0:T(8,128)(2,1)} %param.7), kind=kOutput, calls=%fused_computation.13 | convolution fusion | flops 68719476736 | bytes 100663296 | tf_op jit(solution)/shard_map/dot_general | solution.py:28
  469.5 0.0 all-reduce.3.cloned.1.call-update
  469.5 34.2 %psum.29 = f32[]{:T(128)} all-reduce(f32[]{:T(128)} %get-tuple-element.10), channel_id=1, replica_groups=mesh['tp'=2,'dp'=8] {'tp','dp'}, use_global_device_ids=true, to_apply=%region_7.0 | all-reduce | flops 1 | bytes 8 | tf_op jit(solution)/shard_map/psum | solution.py:26
  504.4 279.2 %all-reduce.5.cloned.1.call-done = f32[4096,2048]{0,1:T(8,128)} async-done(((f32[4096,2048]{0,1:T(8,128)}), f32[4096,2048]{0,1:T(8,128)}) %all-reduce.5.cloned.1.call-update) | async-done | bytes 33554448 | tf_op jit(solution)/shard_map/psum | solution.py:33
  783.5 33.3 %copy.8 = f32[4096,2048]{1,0:T(8,128)} copy(f32[4096,2048]{0,1:T(8,128)} %all-reduce.5.cloned.1.call-done) | data formatting | bytes 67108864
  816.9 1423.0 %all-reduce.3.cloned.1.call-done = f32[4096,4096]{1,0:T(8,128)} async-done(((f32[4096,4096]{1,0:T(8,128)}), f32[4096,4096]{1,0:T(8,128)}) %all-reduce.3.cloned.1.call-update) | async-done | bytes 67108880 | tf_op jit(solution)/shard_map/psum | solution.py:30
  2239.9 44.1 %copy.11 = f32[4096,4096]{1,0:T(8,128)} copy(f32[4096,4096]{1,0:T(8,128)} %all-reduce.3.cloned.1.call-done) | data formatting | bytes 134217728
  (6 shorter events, 0.2 us)
Async XLA Ops:
  7.2 776.4 %all-reduce.5.cloned.1.call-start = ((), (), s32[]{:S(2)}) async-start(), calls=%async_computation.1 | async-start | bytes 67108864 | tf_op jit(solution)/shard_map/psum | solution.py:33
  122.6 114.8 %copy-start.1 = (f32[4096]{0:T(1024)S(1)}, f32[4096]{0:T(1024)}, u32[]{:S(2)}) copy-start(f32[4096]{0:T(1024)} %get-tuple-element.17) | copy-start | bytes 49156
  247.7 20.3 copy-start
  390.0 1849.9 %all-reduce.3.cloned.1.call-start = ((), (), s32[]{:S(2)}) async-start(), calls=%async_computation | async-start | bytes 134217728 | tf_op jit(solution)/shard_map/psum | solution.py:30
Sparse Core Ops, SparseCore 0:
  390.1 393.3 all-reduce.4
  786.6 1453.2 all-reduce.2
where the time goes:
time: 2290 us
  waiting for transfers between devices  1700 us (74%)
  matrix products  388 us (17%)
  local copies, waits for them, and re-layouts  84.2 us (4%)
  blocking collectives  51.4 us (2%)
  other arithmetic  50.3 us (2%)
    psum x1, waiting for transfers between devices, local_step(): dh_student = lax.psum(dh_part, 'tp')  1420 us
    psum x1, waiting for transfers between devices, local_step(): dw_student = lax.psum(dw_part, 'dp')  279 us
    dot_general x1, matrix products, local_step(): jnp.dot(h_student, w_student, preferred_element_type=jnp.float32)  115 us
    dot_general x1, matrix products, local_step(): jnp.dot(h_teacher, w_teacher, preferred_element_type=jnp.float32)  115 us
    unnamed x6, local copies, waits for them, and re-layouts  84 us
    dot_general x1, matrix products, local_step(): lax.dot_general(dz_student, w_student, (((1,), (1,)), ((), ())), preferre...  79.4 us
    dot_general x1, matrix products, local_step(): lax.dot_general(h_student, dz_student, (((0,), (0,)), ((), ())), preferre...  78.3 us
  transfers between devices with their start and end apart: 2, of which 2 were waited for; matrix products, arithmetic and copies ran while one was open for 5% of the time, Pallas kernels for 0%

commit v1 on v0

v1 whole, which is shorter than its diff:
```python
import functools

import jax
import jax.numpy as jnp
from jax import lax
from jax.experimental import pallas as pl
from jax.experimental.pallas import tpu as pltpu
from jax.sharding import PartitionSpec as P


F32 = jnp.float32
BF16 = jnp.bfloat16
BM = 256
FM = 512
CN = 512
LANES = 128
SHARED_BLOCKS = 5
W_PIECES = 2
VMEM_LIMIT = 60 * 1024 * 1024


def _dot(a, b):
    return jnp.dot(a, b, preferred_element_type=F32)


def _fwd_kernel(slot, h_ref, w_ref, prev_ref, *rest):
    z_ref, st_ref = rest[-2:]
    rows = h_ref.shape[0]
    run_max = jnp.full((rows, LANES), -jnp.inf, F32)
    run_sum = jnp.zeros((rows, LANES), F32)
    for c in range(w_ref.shape[1] // CN):
        z = _dot(h_ref[...], w_ref[:, c * CN:(c + 1) * CN])
        z_ref[:, c * CN:(c + 1) * CN] = z
        parts = [z[:, k * LANES:(k + 1) * LANES] for k in range(CN // LANES)]
        new_max = run_max
        for part in parts:
            new_max = jnp.maximum(new_max, part)
        run_sum = run_sum * jnp.exp(run_max - new_max)
        for part in parts:
            run_sum = run_sum + jnp.exp(part - new_max)
        run_max = new_max
    row_max = jnp.max(run_max, axis=1, keepdims=True)
    row_sum = jnp.sum(run_sum * jnp.exp(run_max - row_max), axis=1, keepdims=True)
    lane = lax.broadcasted_iota(jnp.int32, (rows, LANES), 1)
    packed = jnp.where(lane == slot, row_max, jnp.where(lane == slot + 1, row_sum, 0.0))
    st_ref[...] = prev_ref[...] + packed.T[:8, :]


def _row_stats(st_ref):
    a, b = st_ref[0], st_ref[1]
    rows = []
    for k in (0, 2):
        m_a, s_a, m_b, s_b = a[k:k + 1], a[k + 1:k + 2], b[k:k + 1], b[k + 1:k + 2]
        m = jnp.maximum(m_a, m_b)
        s = s_a * jnp.exp(m_a - m) + s_b * jnp.exp(m_b - m)
        rows += [m, 1.0 / s, jnp.log(s)]
    flat = jnp.concatenate(rows + [jnp.zeros((LANES - len(rows), BM), F32)], axis=0)
    cols = flat.T
    return [cols[:, k:k + 1] for k in range(6)]


def _dz_kernel(tok_total, zt_ref, zs_ref, st_ref, *rest):
    dz_ref, share_ref, kl_ref = rest[-3:]
    m_t, r_t, l_t, m_s, r_s, l_s = _row_stats(st_ref)
    kl = jnp.zeros((8, LANES), F32)
    for c in range(zt_ref.shape[1] // CN):
        cs = slice(c * CN, (c + 1) * CN)
        shift_t = zt_ref[:, cs] - m_t
        shift_s = zs_ref[:, cs] - m_s
        p_t = jnp.exp(shift_t) * r_t
        p_s = jnp.exp(shift_s) * r_s
        dz_ref[:, cs] = ((p_s - p_t) * (1.0 / tok_total)).astype(BF16)
        term = p_t * ((shift_t - l_t) - (shift_s - l_s))
        term = term[:, :256] + term[:, 256:]
        term = term[:, :LANES] + term[:, LANES:]
        kl = kl + jnp.sum(term.reshape(BM // 8, 8, LANES), axis=0)

    @pl.when(pl.program_id(0) == 0)
    def _():
        kl_ref[...] = jnp.zeros_like(kl_ref)

    @pl.when(pl.program_id(0) < SHARED_BLOCKS)
    def _():
        share_ref[...] = dz_ref[...].astype(F32)

    kl_ref[...] += kl


def _narrow_kernel(*refs):
    per_piece = pl.num_programs(0) // W_PIECES
    out_ref = refs[-1]
    for j in range(W_PIECES):
        @pl.when(pl.program_id(0) // per_piece == j)
        def _(j=j):
            out_ref[...] = refs[j][...].astype(BF16)


def _far_kernel(tok_total, ht_ref, hs_ref, wt_ref, ws_ref, st_ref, got_ref, kl_in_ref, _, dz_ref, kl_ref):
    i = pl.program_id(0)
    kl_ref[...] = kl_in_ref[...]

    @pl.when(i < SHARED_BLOCKS)
    def _():
        dz_ref[...] = got_ref[...].astype(BF16)

    @pl.when(i >= SHARED_BLOCKS)
    def _():
        m_t, r_t, _, m_s, r_s, _ = _row_stats(st_ref)
        for c in range(dz_ref.shape[1] // CN):
            cs = slice(c * CN, (c + 1) * CN)
            p_t = jnp.exp(_dot(ht_ref[...], wt_ref[:, cs]) - m_t) * r_t
            p_s = jnp.exp(_dot(hs_ref[...], ws_ref[:, cs]) - m_s) * r_s
            dz_ref[:, cs] = ((p_s - p_t) * (1.0 / tok_total)).astype(BF16)


def _resident(shape):
    return pl.BlockSpec(shape, lambda i: (0, 0), pipeline_mode=pl.Buffered(1))


def _untouched():
    return pl.BlockSpec(memory_space=pl.ANY)


def _params():
    return pltpu.CompilerParams(dimension_semantics=("arbitrary",), vmem_limit_bytes=VMEM_LIMIT)


def solution(mesh):
    tp_size, dp_size = mesh.shape["tp"], mesh.shape["dp"]
    swap = [(k, (k + 1) % tp_size) for k in range(tp_size)]

    def local_step(h_teacher, h_student, w_teacher, w_student):
        tokens, depth = h_teacher.shape
        vocab = w_teacher.shape[1]
        tok_total = tokens * dp_size
        blocks = tokens // BM
        shared = SHARED_BLOCKS * BM
        unit = 2 * tokens * depth * vocab

        dp_index = lax.axis_index("dp")
        piece = depth // W_PIECES
        part = piece // dp_size

        def far_slices(w):
            out = []
            for j in range(W_PIECES):
                mine = lax.dynamic_slice_in_dim(w, j * piece + dp_index * part, part, axis=0)
                out.append(lax.ppermute(mine.astype(F32), "tp", swap))
            return out

        def far_gather(slices):
            out = []
            for theirs in slices:
                out.append(lax.all_gather(theirs, "dp", axis=0, tiled=True))
            return out

        def narrow(wide):
            per_piece = piece // BM
            return pl.pallas_call(
                _narrow_kernel,
                grid=(depth // BM,),
                in_specs=[pl.BlockSpec((BM, vocab),
                                       lambda i, j=j: (jnp.clip(i - j * per_piece, 0, per_piece - 1), 0))
                          for j in range(W_PIECES)],
                out_specs=pl.BlockSpec((BM, vocab), lambda i: (i, 0)),
                out_shape=jax.ShapeDtypeStruct((depth, vocab), BF16),
                compiler_params=_params(),
                cost_estimate=pl.CostEstimate(flops=unit // 4, bytes_accessed=48 << 20, transcendentals=0),
                name="narrow",
            )(*wide)

        def forward(slot, h, w, prev, first, count, into=None):
            base = first // FM
            held = [] if into is None else list(into)
            rows = lambda i: (i + base, 0)
            lanes = lambda i: (0, i + base)
            return pl.pallas_call(
                functools.partial(_fwd_kernel, slot),
                grid=(count // FM,),
                in_specs=[pl.BlockSpec((FM, depth), rows),
                          _resident((depth, vocab)),
                          pl.BlockSpec((8, FM), lanes)] + [_untouched()] * len(held),
                out_specs=[pl.BlockSpec((FM, vocab), rows), pl.BlockSpec((8, FM), lanes)],
                out_shape=[jax.ShapeDtypeStruct((tokens, vocab), F32),
                           jax.ShapeDtypeStruct((8, tokens), F32)],
                input_output_aliases={3: 0, 4: 1} if held else {},
                compiler_params=_params(),
                cost_estimate=pl.CostEstimate(flops=unit * count // tokens,
                                              bytes_accessed=(16 << 20) + (64 << 20) * count // tokens,
                                              transcendentals=0),
                name="fwd",
            )(h, w, prev, *held)

        slices_t = far_slices(w_teacher)
        slices_s = far_slices(w_student)
        wide_t = far_gather(slices_t)
        wide_s = far_gather(slices_s)

        none = jnp.zeros((8, tokens), F32)
        half = tokens // 2
        start = forward(0, h_teacher, w_teacher, none, 0, half)
        z_t, stats_t = forward(0, h_teacher, w_teacher, none, half, half, start)
        z_s, stats = forward(2, h_student, w_student, stats_t, 0, tokens)

        both = lax.all_gather(stats, "tp")

        dz_own, share, kl_part = pl.pallas_call(
            functools.partial(_dz_kernel, tok_total),
            grid=(blocks,),
            in_specs=[pl.BlockSpec((BM, vocab), lambda i: (i, 0)),
                      pl.BlockSpec((BM, vocab), lambda i: (i, 0)),
                      pl.BlockSpec((tp_size, 8, BM), lambda i: (0, 0, i))],
            out_specs=[pl.BlockSpec((BM, vocab), lambda i: (i, 0)),
                       pl.BlockSpec((BM, vocab), lambda i: (jnp.minimum(i, SHARED_BLOCKS - 1), 0)),
                       pl.BlockSpec((8, LANES), lambda i: (0, 0))],
            out_shape=[jax.ShapeDtypeStruct((tokens, vocab), BF16),
                       jax.ShapeDtypeStruct((shared, vocab), F32),
                       jax.ShapeDtypeStruct((8, LANES), F32)],
            compiler_params=_params(),
            cost_estimate=pl.CostEstimate(flops=unit // 3, bytes_accessed=90 << 20, transcendentals=0),
            name="dz_own",
        )(z_t, z_s, both)

        got = lax.ppermute(share, "tp", swap)

        dw_part = lax.dot_general(h_student, dz_own, (((0,), (0,)), ((), ())),
                                  preferred_element_type=F32)
        dw_student = lax.psum(dw_part, "dp")

        dh_own = lax.dot_general(dz_own, w_student, (((1,), (1,)), ((), ())),
                                 preferred_element_type=F32)

        far_t = narrow(wide_t)
        far_s = narrow(wide_s)

        dz_far, kl_part = pl.pallas_call(
            functools.partial(_far_kernel, tok_total),
            grid=(blocks,),
            in_specs=[pl.BlockSpec((BM, depth), lambda i: (jnp.maximum(i, SHARED_BLOCKS), 0)),
                      pl.BlockSpec((BM, depth), lambda i: (jnp.maximum(i, SHARED_BLOCKS), 0))]
            + [_resident((depth, vocab))] * 2
            + [pl.BlockSpec((tp_size, 8, BM), lambda i: (0, 0, i)),
               pl.BlockSpec((BM, vocab), lambda i: (jnp.minimum(i, SHARED_BLOCKS - 1), 0)),
               pl.BlockSpec((8, LANES), lambda i: (0, 0)), _untouched()],
            out_specs=[pl.BlockSpec((BM, vocab), lambda i: (i, 0)),
                       pl.BlockSpec((8, LANES), lambda i: (0, 0))],
            out_shape=[jax.ShapeDtypeStruct((tokens, vocab), BF16),
                       jax.ShapeDtypeStruct((8, LANES), F32)],
            compiler_params=_params(),
            cost_estimate=pl.CostEstimate(flops=2 * unit * (blocks - SHARED_BLOCKS) // blocks,
                                          bytes_accessed=112 << 20, transcendentals=0),
            name="dz_far",
        )(h_teacher, h_student, far_t, far_s, both, got, kl_part, dh_own)

        kl_loss = lax.psum(jnp.sum(kl_part), ("tp", "dp")) / tok_total

        dh_student = dh_own + lax.dot_general(dz_far, far_s, (((1,), (1,)), ((), ())),
                                              preferred_element_type=F32)
        return kl_loss, dh_student, dw_student

    return jax.shard_map(
        local_step, mesh=mesh,
        in_specs=(P("dp", None), P("dp", None), P(None, "tp"), P(None, "tp")),
        out_specs=(P(), P("dp", None), P(None, "tp")),
        check_vma=False)
```

time: 2290 us -> 1330 us (0.58)
  waiting for transfers between devices: 1700 us -> 592 us
  Pallas kernels: 0 us -> 379 us
  matrix products: 388 us -> 243 us
  local copies, waits for them, and re-layouts: 84.2 us -> 39.8 us
  other arithmetic: 50.3 us -> 7.74 us
    psum x1 -> x0, waiting for transfers between devices: 1420 us -> none  [local_step(): dh_student = lax.psum(dh_part, 'tp')]
    pallas_call x0 -> x7, Pallas kernels: none -> 379 us  [the longest x3 174 us: forward(): pl.pallas_call(functools.partial(_fwd_kernel, slot), grid=(count // FM,),...]
    all_gather x0 -> x4, waiting for transfers between devices: none -> 295 us  [far_gather(): out.append(lax.all_gather(theirs, 'dp', axis=0, tiled=True))]
    ppermute x0 -> x5, waiting for transfers between devices: none -> 182 us  [the longest x4 182 us: far_slices(): out.append(lax.ppermute(mine.astype(F32), 'tp', swap))]
    psum x1, waiting for transfers between devices: 279 us -> 116 us  [local_step(): dw_student = lax.psum(dw_part, 'dp')]
    dot_general x4 -> x3, matrix products: 388 us -> 243 us  [the longest x1 84.2 us: local_step(): lax.dot_general(dz_far, far_s, (((1,), (1,)), ((), ())), preferred_elemen...]
    unnamed x6 -> x9, local copies, waits for them, and re-layouts: 84 us -> 39.1 us
    convert_element_type x1 -> x2, other arithmetic: 31.6 us -> 6.46 us  [far_slices(): out.append(lax.ppermute(mine.astype(F32), 'tp', swap))]
  transfers between devices with their start and end apart: 2 -> 10, of which waited for: 2 -> 9; matrix products, arithmetic and copies ran while one was open for 5% -> 9% of each run, Pallas kernels for 0% -> 3%
where the time goes in v1:
time: 1330 us; the launch traced here: 1320 us
  waiting for transfers between devices  592 us (45%)
  Pallas kernels  379 us (28%)
  matrix products  243 us (18%)
  blocking collectives  41.1 us (3%)
  local copies, waits for them, and re-layouts  39.8 us (3%)
  between operations  16 us (1%)
    all_gather x4, waiting for transfers between devices, far_gather(): out.append(lax.all_gather(theirs, 'dp', axis=0, tiled=True))  295 us
    ppermute x4, waiting for transfers between devices, far_slices(): out.append(lax.ppermute(mine.astype(F32), 'tp', swap))  182 us
    pallas_call x3, Pallas kernels, forward(): pl.pallas_call(functools.partial(_fwd_kernel, slot), grid=(count // FM,),...  174 us
    pallas_call x1, Pallas kernels, local_step(): pl.pallas_call(functools.partial(_far_kernel, tok_total), grid=(blocks,),...  120 us
    psum x1, waiting for transfers between devices, local_step(): dw_student = lax.psum(dw_part, 'dp')  116 us
    dot_general x1, matrix products, local_step(): lax.dot_general(dz_far, far_s, (((1,), (1,)), ((), ())), preferred_elemen...  84.2 us
    dot_general x1, matrix products, local_step(): lax.dot_general(dz_own, w_student, (((1,), (1,)), ((), ())), preferred_el...  79.7 us
    dot_general x1, matrix products, local_step(): lax.dot_general(h_student, dz_own, (((0,), (0,)), ((), ())), preferred_el...  79.4 us
  transfers between devices with their start and end apart: 10, of which 9 were waited for; matrix products, arithmetic and copies ran while one was open for 9% of the time, Pallas kernels for 3%

profile of v1, /device:TPU:0, one launch (start us, length us, event | category | flops | bytes accessed | tf_op | source)
XLA Modules:
  0.0 1321.5 jit_solution(4128856625489219678)
XLA Ops:
  7.2 0.0 all-reduce.2.cloned.1.call-start
  7.2 0.7 broadcast_in_dim.3.prev_ref
  7.9 45.6 %fwd.3 = (f32[4096,2048]{1,0:T(8,128)}, f32[8,4096]{1,0:T(8,128)}) custom-call(bf16[4096,4096]{1,0:T(8,128)(2,1)} %ht_ref.1, bf16[4096,2048]{1,0:T(8,128)(2,1)} %w_ref.4, f32[8,4096]{1,0:T(8,128)} %broadcast_in_dim.3.prev_ref), custom_call_target="tpu_custom_call" | custom-call | flops 34359738368 | bytes 50331648 | tf_op jit(solution)/shard_map/fwd/pallas_call | solution.py:177
  53.5 45.6 %fwd.4 = (f32[4096,2048]{1,0:T(8,128)}, f32[8,4096]{1,0:T(8,128)}) custom-call(bf16[4096,4096]{1,0:T(8,128)(2,1)} %ht_ref.1, bf16[4096,2048]{1,0:T(8,128)(2,1)} %w_ref.4, f32[8,4096]{1,0:T(8,128)} %broadcast_in_dim.3.prev_ref, f32[4096,2048]{1,0:T(8,128)} %get-tuple-element.14.rest_0_, ...), custom_call_target="tpu_custom_call", output_to_operand_aliasing={{0}: (3, {}), {1}: (4, {})} | custom-call | flops 34359738368 | bytes 50331648 | tf_op jit(solution)/shard_map/fwd/pallas_call | solution.py:177
  99.1 82.8 %fwd.5 = (f32[4096,2048]{1,0:T(8,128)}, f32[8,4096]{1,0:T(8,128)}) custom-call(bf16[4096,4096]{1,0:T(8,128)(2,1)} %hs_ref.1, bf16[4096,2048]{1,0:T(8,128)(2,1)} %w_ref.5, f32[8,4096]{1,0:T(8,128)} %get-tuple-element.16.prev_ref), custom_call_target="tpu_custom_call" | custom-call | flops 68719476736 | bytes 83886080 | tf_op jit(solution)/shard_map/fwd/pallas_call | solution.py:177
  181.9 9.3 all-gather
  191.3 41.1 %dz_own.1 = (bf16[4096,2048]{1,0:T(8,128)(2,1)}, f32[1280,2048]{1,0:T(8,128)}, f32[8,128]{1,0:T(8,128)}) custom-call(f32[4096,2048]{1,0:T(8,128)} %get-tuple-element.18.zt_ref, f32[4096,2048]{1,0:T(8,128)} %get-tuple-element.19.zs_ref, f32[2,8,4096]{2,1,0:T(8,128)} %bitcast.9), custom_call_target="tpu_custom_call" | custom-call | flops 22906492928 | bytes 94371840 | tf_op jit(solution)/shard_map/dz_own/pallas_call | solution.py:207
  232.4 79.4 %convolution_bitcast_fusion = f32[4096,2048]{0,1:T(8,128)} fusion(bf16[4096,2048]{1,0:T(8,128)(2,1)} %get-tuple-element.22, bf16[4096,4096]{1,0:T(8,128)(2,1)} %hs_ref.1), kind=kOutput, calls=%fused_computation.1 | convolution fusion | flops 68719476736 | bytes 83886080 | tf_op jit(solution)/shard_map/dot_general | solution.py:226
  311.8 0.0 all-reduce.2.cloned.1.call-update
  311.8 0.0 all-gather.10.cloned.1.call-start
  311.9 3.2 dynamic-slice_convert_fusion
  315.1 0.2 collective-permute-start.2
  315.2 46.6 %collective-permute-done.2 = f32[256,2048]{1,0:T(8,128)S(1)} collective-permute-done((f32[256,2048]{1,0:T(8,128)S(1)}, f32[256,2048]{1,0:T(8,128)S(1)}, u32[]{:S(2)}, u32[]{:S(2)}) %collective-permute-start.2) | collective-permute-done | bytes 2097184 | tf_op jit(solution)/shard_map/ppermute | solution.py:148
  361.9 0.0 copy-start
  361.9 1.4 copy-done
  363.3 0.0 all-gather.10.cloned.1.call-update
  363.3 0.0 all-gather.12.cloned.1.call-start
  363.3 0.3 collective-permute-start.3
  363.7 46.0 %collective-permute-done.3 = f32[256,2048]{1,0:T(8,128)S(1)} collective-permute-done((f32[256,2048]{1,0:T(8,128)}, f32[256,2048]{1,0:T(8,128)S(1)}, u32[]{:S(2)}, u32[]{:S(2)}) %collective-permute-start.3) | collective-permute-done | bytes 2097184 | tf_op jit(solution)/shard_map/ppermute | solution.py:148
  409.6 0.0 copy-start.1
  409.6 1.3 copy-done.1
  411.0 0.0 all-gather.12.cloned.1.call-update
  411.0 0.0 all-gather.6.cloned.1.call-start
  411.0 3.3 dynamic-slice_convert_fusion.2
  414.3 0.4 collective-permute-start
  414.7 45.0 %collective-permute-done = f32[256,2048]{1,0:T(8,128)S(1)} collective-permute-done((f32[256,2048]{1,0:T(8,128)S(1)}, f32[256,2048]{1,0:T(8,128)S(1)}, u32[]{:S(2)}, u32[]{:S(2)}) %collective-permute-start) | collective-permute-done | bytes 2097184 | tf_op jit(solution)/shard_map/ppermute | solution.py:148
  459.6 0.0 copy-start.2
  459.6 1.3 copy-done.2
  461.0 0.0 all-gather.6.cloned.1.call-update
  461.0 0.0 all-gather.8.cloned.1.call-start
  461.0 0.4 collective-permute-start.1
  461.5 44.3 %collective-permute-done.1 = f32[256,2048]{1,0:T(8,128)S(1)} collective-permute-done((f32[256,2048]{1,0:T(8,128)}, f32[256,2048]{1,0:T(8,128)S(1)}, u32[]{:S(2)}, u32[]{:S(2)}) %collective-permute-start.1) | collective-permute-done | bytes 2097184 | tf_op jit(solution)/shard_map/ppermute | solution.py:148
  505.8 0.0 copy-start.3
  505.8 1.4 copy-done.3
  507.1 0.0 all-gather.8.cloned.1.call-update
  507.2 0.5 collective-permute-start.4
  507.7 79.7 %fusion._ = f32[4096,4096]{1,0:T(8,128)} fusion(bf16[4096,2048]{1,0:T(8,128)(2,1)} %get-tuple-element.22, bf16[4096,2048]{1,0:T(8,128)(2,1)} %w_ref.5), kind=kOutput, calls=%fused_computation.6 | convolution fusion | flops 68719476736 | bytes 100663296 | tf_op jit(solution)/shard_map/dot_general | solution.py:230
  587.3 115.5 %all-reduce.2.cloned.1.call-done = f32[4096,2048]{0,1:T(8,128)} async-done(((f32[4096,2048]{0,1:T(8,128)}), f32[4096,2048]{0,1:T(8,128)}) %all-reduce.2.cloned.1.call-update) | async-done | bytes 33554448 | tf_op jit(solution)/shard_map/psum | solution.py:228
  702.9 33.6 %copy.9 = f32[4096,2048]{1,0:T(8,128)} copy(f32[4096,2048]{0,1:T(8,128)} %all-reduce.2.cloned.1.call-done) | data formatting | bytes 67108864
  736.5 54.2 %all-gather.10.cloned.1.call-done.refs_0_ = f32[2048,2048]{1,0:T(8,128)} async-done(((f32[256,2048]{1,0:T(8,128)}), f32[2048,2048]{1,0:T(8,128)}) %all-gather.10.cloned.1.call-update) | async-done | bytes 16777232 | tf_op jit(solution)/shard_map/all_gather | solution.py:154
  790.7 87.9 %all-gather.12.cloned.1.call-done.refs_1_ = f32[2048,2048]{1,0:T(8,128)} async-done(((f32[256,2048]{1,0:T(8,128)}), f32[2048,2048]{1,0:T(8,128)}) %all-gather.12.cloned.1.call-update) | async-done | bytes 16777232 | tf_op jit(solution)/shard_map/all_gather | solution.py:154
  878.6 22.5 %narrow.3.ws_ref = bf16[4096,2048]{1,0:T(8,128)(2,1)} custom-call(f32[2048,2048]{1,0:T(8,128)} %all-gather.10.cloned.1.call-done.refs_0_, f32[2048,2048]{1,0:T(8,128)} %all-gather.12.cloned.1.call-done.refs_1_), custom_call_target="tpu_custom_call" | custom-call | flops 17179869184 | bytes 50331648 | tf_op jit(solution)/shard_map/narrow/pallas_call | solution.py:159
  901.1 65.2 %all-gather.6.cloned.1.call-done.refs_0_ = f32[2048,2048]{1,0:T(8,128)} async-done(((f32[256,2048]{1,0:T(8,128)}), f32[2048,2048]{1,0:T(8,128)}) %all-gather.6.cloned.1.call-update) | async-done | bytes 16777232 | tf_op jit(solution)/shard_map/all_gather | solution.py:154
  966.3 87.7 %all-gather.8.cloned.1.call-done.refs_1_ = f32[2048,2048]{1,0:T(8,128)} async-done(((f32[256,2048]{1,0:T(8,128)}), f32[2048,2048]{1,0:T(8,128)}) %all-gather.8.cloned.1.call-update) | async-done | bytes 16777232 | tf_op jit(solution)/shard_map/all_gather | solution.py:154
  1054.0 21.9 %narrow.2.wt_ref = bf16[4096,2048]{1,0:T(8,128)(2,1)} custom-call(f32[2048,2048]{1,0:T(8,128)} %all-gather.6.cloned.1.call-done.refs_0_, f32[2048,2048]{1,0:T(8,128)} %all-gather.8.cloned.1.call-done.refs_1_), custom_call_target="tpu_custom_call" | custom-call | flops 17179869184 | bytes 50331648 | tf_op jit(solution)/shard_map/narrow/pallas_call | solution.py:159
  1075.9 0.0 collective-permute-done.4.got_ref
  1075.9 119.6 %dz_far.1 = (bf16[4096,2048]{1,0:T(8,128)(2,1)}, f32[8,128]{1,0:T(8,128)}) custom-call(bf16[4096,4096]{1,0:T(8,128)(2,1)} %ht_ref.1, bf16[4096,4096]{1,0:T(8,128)(2,1)} %hs_ref.1, bf16[4096,2048]{1,0:T(8,128)(2,1)} %narrow.2.wt_ref, bf16[4096,2048]{1,0:T(8,128)(2,1)} %narrow.3.ws_ref, f32[2,8,4096]{2,1,0:T(8,128)} %bitcast.10, ...), custom_call_target="tpu_custom_call" | custom-call | flops 94489280512 | bytes 117440512 | tf_op jit(solution)/shard_map/dz_far/pallas_call | solution.py:236
  1195.5 1.3 reduce_sum.9
  1196.7 84.2 %convolution_add_fusion = f32[4096,4096]{1,0:T(8,128)} fusion(f32[4096,4096]{1,0:T(8,128)} %fusion._, bf16[4096,2048]{1,0:T(8,128)(2,1)} %get-tuple-element.24, bf16[4096,2048]{1,0:T(8,128)(2,1)} %narrow.3.ws_ref), kind=kOutput, calls=%fused_computation | convolution fusion | flops 68736253952 | bytes 167772160 | tf_op jit(solution)/shard_map/dot_general | solution.py:257
  1280.9 31.8 %psum.14 = f32[]{:T(128)} all-reduce(f32[]{:T(128)} %reduce_sum.9), channel_id=1, replica_groups=mesh['tp'=2,'dp'=8] {'tp','dp'}, use_global_device_ids=true, to_apply=%region_1.0 | all-reduce | flops 1 | bytes 8 | tf_op jit(solution)/shard_map/psum | solution.py:255
Async XLA Ops:
  7.2 695.7 %all-reduce.2.cloned.1.call-start = ((), (), s32[]{:S(2)}) async-start(), calls=%async_computation.4 | async-start | bytes 67108864 | tf_op jit(solution)/shard_map/psum | solution.py:228
  311.8 478.9 %all-gather.10.cloned.1.call-start = ((), (), s32[]{:S(2)}) async-start(), calls=%async_computation.2 | async-start | bytes 18874368 | tf_op jit(solution)/shard_map/all_gather | solution.py:154
  315.1 46.8 %collective-permute-start.2 = (f32[256,2048]{1,0:T(8,128)S(1)}, f32[256,2048]{1,0:T(8,128)S(1)}, u32[]{:S(2)}, u32[]{:S(2)}) collective-permute-start(f32[256,2048]{1,0:T(8,128)S(1)} %get-tuple-element.29), channel_id=1, source_target_pairs={{0,8},{8,0},{1,9},{9,1},{2,10},{10,2},{3,11},{11,3},{4,12},{12,4},... | collective-permute-start | bytes 6291464 | tf_op jit(solution)/shard_map/ppermute | solution.py:148
  361.9 1.4 copy-start
  363.3 515.3 %all-gather.12.cloned.1.call-start = ((), (), s32[]{:S(2)}) async-start(), calls=%async_computation.3 | async-start | bytes 18874368 | tf_op jit(solution)/shard_map/all_gather | solution.py:154
  363.3 46.3 %collective-permute-start.3 = (f32[256,2048]{1,0:T(8,128)}, f32[256,2048]{1,0:T(8,128)S(1)}, u32[]{:S(2)}, u32[]{:S(2)}) collective-permute-start(f32[256,2048]{1,0:T(8,128)} %get-tuple-element.28), channel_id=1, source_target_pairs={{0,8},{8,0},{1,9},{9,1},{2,10},{10,2},{3,11},{11,3},{4,12},{12,4},... | collective-permute-start | bytes 6291464 | tf_op jit(solution)/shard_map/ppermute | solution.py:148
  409.6 1.3 copy-start.1
  411.0 555.3 %all-gather.6.cloned.1.call-start = ((), (), s32[]{:S(2)}) async-start(), calls=%async_computation | async-start | bytes 18874368 | tf_op jit(solution)/shard_map/all_gather | solution.py:154
  414.3 45.3 %collective-permute-start = (f32[256,2048]{1,0:T(8,128)S(1)}, f32[256,2048]{1,0:T(8,128)S(1)}, u32[]{:S(2)}, u32[]{:S(2)}) collective-permute-start(f32[256,2048]{1,0:T(8,128)S(1)} %get-tuple-element.31), channel_id=1, source_target_pairs={{0,8},{8,0},{1,9},{9,1},{2,10},{10,2},{3,11},{11,3},{4,12},{12,4},... | collective-permute-start | bytes 6291464 | tf_op jit(solution)/shard_map/ppermute | solution.py:148
  459.6 1.3 copy-start.2
  461.0 593.0 %all-gather.8.cloned.1.call-start = ((), (), s32[]{:S(2)}) async-start(), calls=%async_computation.1 | async-start | bytes 18874368 | tf_op jit(solution)/shard_map/all_gather | solution.py:154
  461.0 44.7 %collective-permute-start.1 = (f32[256,2048]{1,0:T(8,128)}, f32[256,2048]{1,0:T(8,128)S(1)}, u32[]{:S(2)}, u32[]{:S(2)}) collective-permute-start(f32[256,2048]{1,0:T(8,128)} %get-tuple-element.30), channel_id=1, source_target_pairs={{0,8},{8,0},{1,9},{9,1},{2,10},{10,2},{3,11},{11,3},{4,12},{12,4},... | collective-permute-start | bytes 6291464 | tf_op jit(solution)/shard_map/ppermute | solution.py:148
  505.8 1.4 copy-start.3
  507.2 568.7 %collective-permute-start.4 = (f32[1280,2048]{1,0:T(8,128)}, f32[1280,2048]{1,0:T(8,128)}, u32[]{:S(2)}, u32[]{:S(2)}) collective-permute-start(f32[1280,2048]{1,0:T(8,128)} %get-tuple-element.20), channel_id=1, source_target_pairs={{0,8},{8,0},{1,9},{9,1},{2,10},{10,2},{3,11},{11,3},{4,12},{12,4},... | collective-permute-start | bytes 31457288 | tf_op jit(solution)/shard_map/ppermute | solution.py:224
Sparse Core Ops, SparseCore 0:
  311.9 390.8 all-reduce.1
  704.7 85.9 all-gather.9
  792.6 85.9 all-gather.11
  880.3 85.9 all-gather.5
  968.0 85.9 all-gather.7
